TPU v7x, 32 devices: a whole 2x2x4 slice. The times are simulated.
32 devices in a mesh: date: 16 (over z, y, x), pix: 2 (over core).
Axes of the slice: x: 2, y: 2, z: 4, core: 2. Of those that a mesh axis runs over, the one named last changes fastest.
Arguments:
- reflect: bfloat16 [64, 6, 16384], P('date', None, 'pix'), may hold values from -8 to 8
- cloud_free: int32 [64, 16384], P('date', 'pix'), may hold values from 0 to 1, as said below
- days: int32 [64], P('date'), may hold values from 1 to 2079, as said below
Outputs:
- median: float32 [6, 16384], P(None, 'pix')
- slope: float32 [6, 16384], P(None, 'pix')
Inputs may be any that keep to these rules, and one draw needn't show every extreme that they name: `cloud_free`: every pixel is clear on at least one of the first 32 dates and on at least one of the others; clear shares differ between tiles. `days`: strictly increasing.
All inputs are finite; a program needn't handle non-finite values.
Results may differ from a plain program's by a relative error of at most 0.0003.
Values may be sent and summed in bfloat16 or wider, within the bound.
A program may use at most 64 MiB of HBM per device.

v0:
```python
import jax
import jax.numpy as jnp
from jax import lax
from jax.sharding import PartitionSpec as P

ridge = 1.0
sentinel = 100.0


def count_ranks(carry, own, piece):

    def step(i, state):
        less, equal, count = state
        other = lax.dynamic_index_in_dim(piece, i, 0, keepdims=True).astype(jnp.float32)
        less = less + (other < own).astype(jnp.float32)
        equal = equal + (other == own).astype(jnp.float32)
        count = count + (other[0, 0] < 50.0).astype(jnp.float32)
        return (less, equal, count)

    return lax.fori_loop(0, piece.shape[0], step, carry)


def select_sums(values, valid, less, equal, count):
    lower = jnp.floor((count - 1.0) / 2.0)
    upper = jnp.floor(count / 2.0)
    low_pick = valid[:, None, :] * ((less <= lower) & (lower < less + equal)).astype(jnp.float32)
    high_pick = valid[:, None, :] * ((less <= upper) & (upper < less + equal)).astype(jnp.float32)
    return (
        jnp.sum(low_pick * values, 0),
        jnp.sum(low_pick, 0),
        jnp.sum(high_pick * values, 0),
        jnp.sum(high_pick, 0),
    )


def finish_median(low_num, low_den, high_num, high_den):
    return 0.5 * (low_num / jnp.maximum(low_den, 1.0) + high_num / jnp.maximum(high_den, 1.0))


def column_median(moved):
    column = moved.astype(jnp.float32)
    column_valid = (column[:, 0, :] < 50.0).astype(jnp.float32)
    zeros = jnp.zeros(column.shape, jnp.float32)
    start_carry = (zeros, zeros, jnp.zeros((column.shape[2],), jnp.float32))
    less, equal, count = count_ranks(start_carry, column, moved)
    low_num, low_den, high_num, high_den = select_sums(column, column_valid, less, equal, count)
    return (column, column_valid, finish_median(low_num, low_den, high_num, high_den))


def fit_slope(s_zero, s_one, s_two, s_y, s_ty):
    first = s_zero + ridge
    determinant = first * (s_two + ridge) - s_one * s_one
    return (first[None, :] * s_ty - s_one[None, :] * s_y) / determinant[None, :]


def local(reflect, cloud_free, days):
    values = reflect.astype(jnp.float32)
    valid = cloud_free.astype(jnp.float32)
    years = days.astype(jnp.float32) / 365.0
    csum = jnp.sum(values * valid[:, None, :], 2)
    cnt = jnp.sum(valid, 1)
    csum, cnt = lax.psum((csum, cnt), "pix")
    scene_mean = csum / jnp.maximum(cnt, 1.0)[:, None]
    marked = jnp.where(valid[:, None, :] > 0, values, sentinel).astype(jnp.bfloat16)
    shifted = values - scene_mean[:, :, None]
    weighted = valid[:, None, :] * shifted
    s_zero = jnp.sum(valid, 0)
    s_one = jnp.sum(years[:, None] * valid, 0)
    s_two = jnp.sum((years * years)[:, None] * valid, 0)
    s_y = jnp.sum(weighted, 0)
    s_ty = jnp.sum(years[:, None, None] * weighted, 0)
    moved = lax.all_to_all(marked, "date", split_axis=2, concat_axis=0, tiled=True)
    column, column_valid, part_median = column_median(moved)
    median = lax.all_gather(part_median, "date", axis=1, tiled=True)
    s_y, s_ty, s_zero, s_one, s_two = lax.psum((s_y, s_ty, s_zero, s_one, s_two), "date")
    slope = fit_slope(s_zero, s_one, s_two, s_y, s_ty)
    return (median, slope)


def solution(mesh):
    placed = (P("date", None, "pix"), P("date", "pix"), P("date"))
    return jax.shard_map(
        local,
        mesh=mesh,
        in_specs=placed,
        out_specs=(P(None, "pix"), P(None, "pix")),
        check_vma=False,
    )
```

profile of v0, /device:TPU:0, one launch (start us, length us, event | category | flops | bytes accessed | tf_op | source)
XLA Modules:
  0.0 414.7 jit_solution(17819752993265104546)
XLA Ops:
  7.9 1.8 convert_reduce_fusion.1
  9.7 0.9 convert_element_type.50
  10.7 1.0 broadcast_compare_fusion
  11.6 1.3 fusion.4
  12.9 2.6 all-reduce.2
  15.6 3.0 fusion.8
  18.6 8.5 %copy.37 = bf16[4,6,8192]{1,0,2:T(4,128)(2,1)} copy(bf16[4,6,8192]{2,0,1:T(4,128)(2,1)S(1)} %get-tuple-element.172) | data formatting | bytes 786432 | tf_op jit(solution)/shard_map/convert_element_type | solution.py:64
  27.2 14.3 %reshape.24 = bf16[16,2,6144]{2,1,0:T(2,128)(2,1)} reshape(bf16[8192,4,6]{2,1,0:T(4,128)(2,1)} %bitcast.17) | data formatting | bytes 786432
  41.5 8.2 %all-to-all-start = ((bf16[16,2,6144]{2,1,0:T(2,128)(2,1)}), bf16[16,2,6144]{2,1,0:T(2,128)(2,1)S(1)}, u32[]{:S(2)}, u32[]{:S(2)}) async-start(bf16[16,2,6144]{2,1,0:T(2,128)(2,1)} %reshape.24), calls=%async_computation | async-start | bytes 786432 | tf_op jit(solution)/shard_map/all_to_all | solution.py:72
  49.7 72.8 %all-reduce.6.cloned.1.call-done = (f32[8192]{0:T(1024)}, f32[8192]{0:T(1024)}, f32[8192]{0:T(1024)}) async-done(((f32[8192]{0:T(1024)}, f32[8192]{0:T(1024)}, f32[8192]{0:T(1024)}), (f32[8192]{0:T(1024)}, f32[8192]{0:T(1024)}, f32[8192]{0:T(1024)})) %all-reduce.6.cloned.1.call-update) | async-done | bytes 98320 | tf_op jit(solution)/shard_map/psum | solution.py:75
  122.5 0.8 broadcast_add_fusion
  123.4 114.3 %all-reduce.8.cloned.1.call-done = (f32[6,8192]{1,0:T(8,128)}, f32[6,8192]{1,0:T(8,128)}) async-done(((f32[6,8192]{1,0:T(8,128)}, f32[6,8192]{1,0:T(8,128)}), (f32[6,8192]{1,0:T(8,128)}, f32[6,8192]{1,0:T(8,128)})) %all-reduce.8.cloned.1.call-update) | async-done | bytes 393232 | tf_op jit(solution)/shard_map/psum | solution.py:75
  237.7 1.8 subtract_divide_fusion
  239.5 20.0 %reshape.25 = bf16[8192,4,6]{2,1,0:T(4,128)(2,1)} reshape(bf16[16,2,6144]{2,1,0:T(2,128)(2,1)S(1)} %all-to-all-done) | data formatting | bytes 786432
  259.5 12.9 %copy.38 = bf16[16,4,6,512]{3,2,1,0:T(8,128)(2,1)} copy(bf16[16,4,6,512]{2,1,3,0:T(4,128)(2,1)} %bitcast.18) | data formatting | bytes 786432 | tf_op jit(solution)/shard_map/all_to_all | solution.py:72
  272.3 1.2 bitcast_convert_fusion
  273.7 91.0 %while.18 = (s32[]{:T(128)}, f32[64,6,512]{2,1,0:T(8,128)S(1)}, f32[64,6,512]{2,1,0:T(8,128)S(1)}, f32[512]{0:T(512)S(1)}, bf16[64,6,512]{2,1,0:T(8,128)(2,1)}, ...) while((s32[]{:T(128)}, f32[64,6,512]{2,1,0:T(8,128)S(1)}, f32[64,6,512]{2,1,0:T(8,128)S(1)}, ...), condition=%wide.region_1.0_spmd.clone, body=%wide.region_0.0_spmd.clone.sunk | while | flops 1577987 | bytes 3985508 | solution.py:20
  273.7 0.7 dynamic-slice_convert_fusion.2
  275.1 0.7 dynamic-slice_convert_fusion.2
  276.5 0.7 dynamic-slice_convert_fusion.2
  277.9 0.7 dynamic-slice_convert_fusion.2
  279.4 0.7 dynamic-slice_convert_fusion.2
  280.8 0.7 dynamic-slice_convert_fusion.2
  282.2 0.7 dynamic-slice_convert_fusion.2
  283.6 0.7 dynamic-slice_convert_fusion.2
  289.3 0.7 dynamic-slice_convert_fusion.2
  290.7 0.7 dynamic-slice_convert_fusion.2
  292.2 0.7 dynamic-slice_convert_fusion.2
  293.6 0.7 dynamic-slice_convert_fusion.2
  295.0 0.7 dynamic-slice_convert_fusion.2
  365.1 1.6 fusion.1
  366.8 40.4 %all_gather.3 = f32[6,8192]{1,0:T(8,128)S(1)} all-gather(f32[6,512]{1,0:T(8,128)S(1)} %add_multiply_fusion), channel_id=1, replica_groups=mesh['date'=16,'pix'=2] {'date'}, dimensions={1}, use_global_device_ids=true | all-gather | bytes 208896 | tf_op jit(solution)/shard_map/all_gather | solution.py:74
  (260 shorter events, 82.1 us)
Async XLA Ops:
  7.2 115.4 %all-reduce.6.cloned.1.call-start = ((), (), s32[]{:S(2)}) async-start(), calls=%async_computation.1 | async-start | bytes 196608 | tf_op jit(solution)/shard_map/psum | solution.py:75
  9.7 228.0 %all-reduce.8.cloned.1.call-start = ((), (), s32[]{:S(2)}) async-start(), calls=%async_computation.2 | async-start | bytes 1048576 | tf_op jit(solution)/shard_map/psum | solution.py:75
  41.5 198.0 %all-to-all-start = ((bf16[16,2,6144]{2,1,0:T(2,128)(2,1)}), bf16[16,2,6144]{2,1,0:T(2,128)(2,1)S(1)}, u32[]{:S(2)}, u32[]{:S(2)}) async-start(bf16[16,2,6144]{2,1,0:T(2,128)(2,1)} %reshape.24), calls=%async_computation | async-start | bytes 786432 | tf_op jit(solution)/shard_map/all_to_all | solution.py:72
Sparse Core Ops, SparseCore 0:
  13.8 108.7 all-reduce.5
  128.3 109.3 all-reduce.7
where the time goes:
time: 419 us; the launch traced here: 415 us
  waiting for transfers between devices  187 us (45%)
  other arithmetic  104 us (25%)
  local copies, waits for them, and re-layouts  56.4 us (13%)
  blocking collectives  43 us (10%)
  between operations  14.1 us (3%)
  starting transfers between devices  8.26 us (2%)
    psum x2, waiting for transfers between devices, local(): lax.psum((s_y, s_ty, s_zero, s_one, s_two), 'date')  187 us
    convert_element_type x64, other arithmetic, step(): lax.dynamic_index_in_dim(piece, i, 0, keepdims=True).astype(jnp.float32)  45.1 us
    add x64, other arithmetic, step(): equal = equal + (other == own).astype(jnp.float32)  42.9 us
    all_gather x1, blocking collectives, local(): median = lax.all_gather(part_median, 'date', axis=1, tiled=True)  40.4 us
    unnamed x4, local copies, waits for them, and re-layouts  35 us
    all_to_all x1, local copies, waits for them, and re-layouts, local(): lax.all_to_all(marked, 'date', split_axis=2, concat_axis=0, tiled=True)  12.9 us
    convert_element_type x1, local copies, waits for them, and re-layouts, local(): jnp.where(valid[:, None, :] > 0, values, sentinel).astype(jnp.bfloat16)  8.54 us
  transfers between devices with their start and end apart: 3, of which 2 were waited for; matrix products, arithmetic and copies ran while one was open for 8% of the time, Pallas kernels for 0%

commit v1 on v0

--- a/solution.py
+++ b/solution.py
@@ -69,7 +69,9 @@
     s_two = jnp.sum((years * years)[:, None] * valid, 0)
     s_y = jnp.sum(weighted, 0)
     s_ty = jnp.sum(years[:, None, None] * weighted, 0)
-    moved = lax.all_to_all(marked, "date", split_axis=2, concat_axis=0, tiled=True)
+    parts = jnp.split(marked, lax.axis_size("date"), axis=2)
+    arrived = lax.all_to_all(jnp.stack(parts), "date", 0, 0)
+    moved = jnp.concatenate(arrived, axis=0)
     column, column_valid, part_median = column_median(moved)
     median = lax.all_gather(part_median, "date", axis=1, tiled=True)
     s_y, s_ty, s_zero, s_one, s_two = lax.psum((s_y, s_ty, s_zero, s_one, s_two), "date")

time: 419 us -> 385 us (0.919)
  local copies, waits for them, and re-layouts: 56.4 us -> 11.8 us
  waiting for transfers between devices: 187 us -> 204 us
  other arithmetic: 104 us -> 98.1 us
    unnamed x4 -> x27, local copies, waits for them, and re-layouts: 35 us -> 11.1 us
    psum x2, waiting for transfers between devices: 187 us -> 204 us  [local(): lax.psum((s_y, s_ty, s_zero, s_one, s_two), 'date')]
    all_to_all x1, local copies, waits for them, and re-layouts: 12.9 us -> 0.09 us  [local(): arrived = lax.all_to_all(jnp.stack(parts), 'date', 0, 0)]
    convert_element_type x1 -> x0, local copies, waits for them, and re-layouts: 8.54 us -> none  [local(): jnp.where(valid[:, None, :] > 0, values, sentinel).astype(jnp.bfloat16)]
  transfers between devices with their start and end apart: 3 -> 3, of which waited for: 2 -> 2; matrix products, arithmetic and copies ran while one was open for 8% -> 4% of each run, Pallas kernels for 0% -> 0%
where the time goes in v1:
time: 385 us; the launch traced here: 381 us
  waiting for transfers between devices  204 us (53%)
  other arithmetic  98.1 us (25%)
  blocking collectives  43 us (11%)
  between operations  14.2 us (4%)
  local copies, waits for them, and re-layouts  11.8 us (3%)
  starting transfers between devices  8.26 us (2%)
    psum x2, waiting for transfers between devices, local(): lax.psum((s_y, s_ty, s_zero, s_one, s_two), 'date')  204 us
    convert_element_type x64, other arithmetic, step(): lax.dynamic_index_in_dim(piece, i, 0, keepdims=True).astype(jnp.float32)  45.1 us
    add x64, other arithmetic, step(): equal = equal + (other == own).astype(jnp.float32)  42.9 us
    all_gather x1, blocking collectives, local(): median = lax.all_gather(part_median, 'date', axis=1, tiled=True)  40.4 us
    unnamed x27, local copies, waits for them, and re-layouts  11.1 us
    all_to_all x1, starting transfers between devices, local(): arrived = lax.all_to_all(jnp.stack(parts), 'date', 0, 0)  8.18 us
  transfers between devices with their start and end apart: 3, of which 2 were waited for; matrix products, arithmetic and copies ran while one was open for 4% of the time, Pallas kernels for 0%

profile of v1, /device:TPU:0, one launch (start us, length us, event | category | flops | bytes accessed | tf_op | source)
XLA Modules:
  0.0 380.8 jit_solution(10285455160166653592)
XLA Ops:
  7.2 0.7 fusion.9
  7.9 1.8 convert_reduce_fusion.1
  10.2 2.6 all-reduce.2
  12.9 2.0 fusion.8
  24.7 8.2 %all-to-all-start = ((bf16[16,4,6,512]{3,1,2,0:T(4,128)(2,1)}), bf16[16,4,6,512]{3,1,2,0:T(4,128)(2,1)S(1)}, u32[]{:S(2)}, u32[]{:S(2)}) async-start(bf16[16,4,6,512]{3,1,2,0:T(4,128)(2,1)} %constant_dynamic-update-slice_fusion), calls=%async_computation | async-start | bytes 786432 | tf_op jit(solution)/shard_map/all_to_all | solution.py:73
  32.9 89.7 %all-reduce.6.cloned.1.call-done = (f32[8192]{0:T(1024)}, f32[8192]{0:T(1024)}, f32[8192]{0:T(1024)}) async-done(((f32[8192]{0:T(1024)}, f32[8192]{0:T(1024)}, f32[8192]{0:T(1024)}), (f32[8192]{0:T(1024)}, f32[8192]{0:T(1024)}, f32[8192]{0:T(1024)})) %all-reduce.6.cloned.1.call-update) | async-done | bytes 98320 | tf_op jit(solution)/shard_map/psum | solution.py:77
  122.6 0.8 broadcast_add_fusion
  123.4 114.3 %all-reduce.8.cloned.1.call-done = (f32[6,8192]{1,0:T(8,128)}, f32[6,8192]{1,0:T(8,128)}) async-done(((f32[6,8192]{1,0:T(8,128)}, f32[6,8192]{1,0:T(8,128)}), (f32[6,8192]{1,0:T(8,128)}, f32[6,8192]{1,0:T(8,128)})) %all-reduce.8.cloned.1.call-update) | async-done | bytes 393232 | tf_op jit(solution)/shard_map/psum | solution.py:77
  237.7 1.8 subtract_divide_fusion
  240.6 90.5 %while.18 = (s32[]{:T(128)}, f32[64,6,512]{2,1,0:T(8,128)S(1)}, f32[64,6,512]{2,1,0:T(8,128)S(1)}, f32[512]{0:T(512)S(1)}, bf16[64,6,512]{2,1,0:T(8,128)(2,1)}, ...) while((s32[]{:T(128)}, f32[64,6,512]{2,1,0:T(8,128)S(1)}, f32[64,6,512]{2,1,0:T(8,128)S(1)}, ...), condition=%wide.region_1.0_spmd.clone, body=%wide.region_0.0_spmd.clone.sunk | while | flops 1577987 | bytes 3985516 | solution.py:20
  240.6 0.7 dynamic-slice_convert_fusion.2
  243.4 0.7 dynamic-slice_convert_fusion.2
  244.8 0.7 dynamic-slice_convert_fusion.2
  246.3 0.7 dynamic-slice_convert_fusion.2
  247.7 0.7 dynamic-slice_convert_fusion.2
  249.1 0.7 dynamic-slice_convert_fusion.2
  251.9 0.7 dynamic-slice_convert_fusion.2
  253.3 0.7 dynamic-slice_convert_fusion.2
  254.7 0.7 dynamic-slice_convert_fusion.2
  256.2 0.7 dynamic-slice_convert_fusion.2
  257.6 0.7 dynamic-slice_convert_fusion.2
  260.4 0.7 dynamic-slice_convert_fusion.2
  261.8 0.7 dynamic-slice_convert_fusion.2
  263.2 0.7 dynamic-slice_convert_fusion.2
  264.6 0.7 dynamic-slice_convert_fusion.2
  266.1 0.7 dynamic-slice_convert_fusion.2
  267.5 0.7 dynamic-slice_convert_fusion.2
  270.3 0.7 dynamic-slice_convert_fusion.2
  271.7 0.7 dynamic-slice_convert_fusion.2
  273.1 0.7 dynamic-slice_convert_fusion.2
  274.5 0.7 dynamic-slice_convert_fusion.2
  332.8 40.4 %all_gather.3 = f32[6,8192]{1,0:T(8,128)S(1)} all-gather(f32[6,512]{1,0:T(8,128)S(1)} %add_multiply_fusion), channel_id=1, replica_groups=mesh['date'=16,'pix'=2] {'date'}, dimensions={1}, use_global_device_ids=true | all-gather | bytes 208896 | tf_op jit(solution)/shard_map/all_gather | solution.py:76
  (283 shorter events, 88.1 us)
Async XLA Ops:
  7.2 2.7 copy-start.3
  7.2 2.8 copy-start.2
  7.2 115.4 %all-reduce.6.cloned.1.call-start = ((), (), s32[]{:S(2)}) async-start(), calls=%async_computation.1 | async-start | bytes 196608 | tf_op jit(solution)/shard_map/psum | solution.py:77
  9.8 227.9 %all-reduce.8.cloned.1.call-start = ((), (), s32[]{:S(2)}) async-start(), calls=%async_computation.2 | async-start | bytes 1048576 | tf_op jit(solution)/shard_map/psum | solution.py:77
  24.7 214.8 %all-to-all-start = ((bf16[16,4,6,512]{3,1,2,0:T(4,128)(2,1)}), bf16[16,4,6,512]{3,1,2,0:T(4,128)(2,1)S(1)}, u32[]{:S(2)}, u32[]{:S(2)}) async-start(bf16[16,4,6,512]{3,1,2,0:T(4,128)(2,1)} %constant_dynamic-update-slice_fusion), calls=%async_computation | async-start | bytes 786432 | tf_op jit(solution)/shard_map/all_to_all | solution.py:73
  122.6 115.2 %copy-start.4 = (f32[8192]{0:T(1024)S(1)}, f32[8192]{0:T(1024)}, u32[]{:S(2)}) copy-start(f32[8192]{0:T(1024)} %get-tuple-element.159) | copy-start | bytes 98308
  239.6 0.8 copy-start
  331.1 1.0 copy-start.1
Sparse Core Ops, SparseCore 0:
  13.8 108.7 all-reduce.5
  128.3 109.3 all-reduce.7

commit v2 on v0

--- a/solution.py
+++ b/solution.py
@@ -71,7 +71,8 @@
     s_ty = jnp.sum(years[:, None, None] * weighted, 0)
     moved = lax.all_to_all(marked, "date", split_axis=2, concat_axis=0, tiled=True)
     column, column_valid, part_median = column_median(moved)
-    median = lax.all_gather(part_median, "date", axis=1, tiled=True)
+    kept_arr = lax.all_gather(part_median, axis_name="date")
+    median = jnp.concatenate(kept_arr, 1)
     s_y, s_ty, s_zero, s_one, s_two = lax.psum((s_y, s_ty, s_zero, s_one, s_two), "date")
     slope = fit_slope(s_zero, s_one, s_two, s_y, s_ty)
     return (median, slope)

time: 419 us -> 419 us (level)
  no operation moved by 1% of the time
where the time goes in v2:
time: 419 us; the launch traced here: 415 us
  waiting for transfers between devices  187 us (45%)
  other arithmetic  104 us (25%)
  local copies, waits for them, and re-layouts  56.4 us (13%)
  blocking collectives  43 us (10%)
  between operations  14.1 us (3%)
  starting transfers between devices  8.26 us (2%)
    psum x2, waiting for transfers between devices, local(): lax.psum((s_y, s_ty, s_zero, s_one, s_two), 'date')  187 us
    convert_element_type x64, other arithmetic, step(): lax.dynamic_index_in_dim(piece, i, 0, keepdims=True).astype(jnp.float32)  45.1 us
    add x64, other arithmetic, step(): equal = equal + (other == own).astype(jnp.float32)  42.9 us
    all_gather x1, blocking collectives, local(): kept_arr = lax.all_gather(part_median, axis_name='date')  40.4 us
    unnamed x4, local copies, waits for them, and re-layouts  35 us
    all_to_all x1, local copies, waits for them, and re-layouts, local(): lax.all_to_all(marked, 'date', split_axis=2, concat_axis=0, tiled=True)  12.9 us
    convert_element_type x1, local copies, waits for them, and re-layouts, local(): jnp.where(valid[:, None, :] > 0, values, sentinel).astype(jnp.bfloat16)  8.54 us
  transfers between devices with their start and end apart: 3, of which 2 were waited for; matrix products, arithmetic and copies ran while one was open for 8% of the time, Pallas kernels for 0%

profile of v2, /device:TPU:0, one launch (start us, length us, event | category | flops | bytes accessed | tf_op | source)
XLA Modules:
  0.0 414.7 jit_solution(1926943859644261276)
XLA Ops:
  7.9 1.8 convert_reduce_fusion.1
  9.7 0.9 convert_element_type.50
  10.7 1.0 broadcast_compare_fusion
  11.6 1.3 fusion.4
  12.9 2.6 all-reduce.2
  15.6 3.0 fusion.8
  18.6 8.5 %copy.37 = bf16[4,6,8192]{1,0,2:T(4,128)(2,1)} copy(bf16[4,6,8192]{2,0,1:T(4,128)(2,1)S(1)} %get-tuple-element.172) | data formatting | bytes 786432 | tf_op jit(solution)/shard_map/convert_element_type | solution.py:64
  27.2 14.3 %reshape.79 = bf16[16,2,6144]{2,1,0:T(2,128)(2,1)} reshape(bf16[8192,4,6]{2,1,0:T(4,128)(2,1)} %bitcast.22) | data formatting | bytes 786432
  41.5 8.2 %all-to-all-start = ((bf16[16,2,6144]{2,1,0:T(2,128)(2,1)}), bf16[16,2,6144]{2,1,0:T(2,128)(2,1)S(1)}, u32[]{:S(2)}, u32[]{:S(2)}) async-start(bf16[16,2,6144]{2,1,0:T(2,128)(2,1)} %reshape.79), calls=%async_computation | async-start | bytes 786432 | tf_op jit(solution)/shard_map/all_to_all | solution.py:72
  49.7 72.8 %all-reduce.6.cloned.1.call-done = (f32[8192]{0:T(1024)}, f32[8192]{0:T(1024)}, f32[8192]{0:T(1024)}) async-done(((f32[8192]{0:T(1024)}, f32[8192]{0:T(1024)}, f32[8192]{0:T(1024)}), (f32[8192]{0:T(1024)}, f32[8192]{0:T(1024)}, f32[8192]{0:T(1024)})) %all-reduce.6.cloned.1.call-update) | async-done | bytes 98320 | tf_op jit(solution)/shard_map/psum | solution.py:76
  122.5 0.8 broadcast_add_fusion
  123.4 114.3 %all-reduce.8.cloned.1.call-done = (f32[6,8192]{1,0:T(8,128)}, f32[6,8192]{1,0:T(8,128)}) async-done(((f32[6,8192]{1,0:T(8,128)}, f32[6,8192]{1,0:T(8,128)}), (f32[6,8192]{1,0:T(8,128)}, f32[6,8192]{1,0:T(8,128)})) %all-reduce.8.cloned.1.call-update) | async-done | bytes 393232 | tf_op jit(solution)/shard_map/psum | solution.py:76
  237.7 1.8 subtract_divide_fusion
  239.5 20.0 %reshape.80 = bf16[8192,4,6]{2,1,0:T(4,128)(2,1)} reshape(bf16[16,2,6144]{2,1,0:T(2,128)(2,1)S(1)} %all-to-all-done) | data formatting | bytes 786432
  259.5 12.9 %copy.38 = bf16[16,4,6,512]{3,2,1,0:T(8,128)(2,1)} copy(bf16[16,4,6,512]{2,1,3,0:T(4,128)(2,1)} %bitcast.23) | data formatting | bytes 786432 | tf_op jit(solution)/shard_map/all_to_all | solution.py:72
  272.3 1.2 bitcast_convert_fusion
  273.7 90.9 %while.18 = (s32[]{:T(128)}, f32[64,6,512]{2,1,0:T(8,128)S(1)}, f32[64,6,512]{2,1,0:T(8,128)S(1)}, f32[512]{0:T(512)S(1)}, bf16[64,6,512]{2,1,0:T(8,128)(2,1)}, ...) while((s32[]{:T(128)}, f32[64,6,512]{2,1,0:T(8,128)S(1)}, f32[64,6,512]{2,1,0:T(8,128)S(1)}, ...), condition=%wide.region_1.0_spmd.clone, body=%wide.region_0.0_spmd.clone.sunk | while | flops 1577987 | bytes 3985508 | solution.py:20
  273.7 0.7 dynamic-slice_convert_fusion.2
  275.1 0.7 dynamic-slice_convert_fusion.2
  276.5 0.7 dynamic-slice_convert_fusion.2
  277.9 0.7 dynamic-slice_convert_fusion.2
  280.8 0.7 dynamic-slice_convert_fusion.2
  282.2 0.7 dynamic-slice_convert_fusion.2
  283.6 0.7 dynamic-slice_convert_fusion.2
  285.1 0.7 dynamic-slice_convert_fusion.2
  286.5 0.7 dynamic-slice_convert_fusion.2
  287.9 0.7 dynamic-slice_convert_fusion.2
  289.3 0.7 dynamic-slice_convert_fusion.2
  292.2 0.7 dynamic-slice_convert_fusion.2
  293.6 0.7 dynamic-slice_convert_fusion.2
  365.1 1.6 fusion.1
  366.8 40.4 %all-gather.1 = f32[16,6,512]{2,1,0:T(8,128)S(1)} all-gather(f32[1,6,512]{2,1,0:T(8,128)S(1)} %multiply_bitcast_fusion), channel_id=2, replica_groups=mesh['date'=16,'pix'=2] {'date'}, dimensions={0}, use_global_device_ids=true | all-gather | bytes 208896 | tf_op jit(solution)/shard_map/all_gather | solution.py:74
  (260 shorter events, 82.1 us)
Async XLA Ops:
  7.2 115.4 %all-reduce.6.cloned.1.call-start = ((), (), s32[]{:S(2)}) async-start(), calls=%async_computation.1 | async-start | bytes 196608 | tf_op jit(solution)/shard_map/psum | solution.py:76
  9.7 228.0 %all-reduce.8.cloned.1.call-start = ((), (), s32[]{:S(2)}) async-start(), calls=%async_computation.2 | async-start | bytes 1048576 | tf_op jit(solution)/shard_map/psum | solution.py:76
  41.5 198.0 %all-to-all-start = ((bf16[16,2,6144]{2,1,0:T(2,128)(2,1)}), bf16[16,2,6144]{2,1,0:T(2,128)(2,1)S(1)}, u32[]{:S(2)}, u32[]{:S(2)}) async-start(bf16[16,2,6144]{2,1,0:T(2,128)(2,1)} %reshape.79), calls=%async_computation | async-start | bytes 786432 | tf_op jit(solution)/shard_map/all_to_all | solution.py:72
Sparse Core Ops, SparseCore 0:
  13.8 108.7 all-reduce.5
  128.3 109.3 all-reduce.7
